TPU v7x, 32 devices: a whole 2x2x4 slice. The times are simulated.
32 devices in a mesh: coarse: 2 (over y), fine: 4 (over z), model: 4 (over x, core).
Axes of the slice: x: 2, y: 2, z: 4, core: 2. Of those that a mesh axis runs over, the one named last changes fastest.
Arguments:
- fresh_keys: bfloat16 [8, 12288, 8, 128], P(None, ('coarse', 'fine'), 'model'), may hold values from -6 to 6
- fresh_values: bfloat16 [8, 12288, 8, 128], P(None, ('coarse', 'fine'), 'model'), may hold values from -6 to 6
- turn_angle: float32 [12288, 64], replicated, may hold values from -3.140625 to 3.140625
Outputs:
- cache_keys: bfloat16 [8, 12288, 8, 128], P(('coarse', 'fine'), None, 'model')
- cache_values: bfloat16 [8, 12288, 8, 128], P(('coarse', 'fine'), None, 'model')
- page_high: bfloat16 [8, 384, 8, 128], P(('coarse', 'fine'), None, 'model')
- page_low: bfloat16 [8, 384, 8, 128], P(('coarse', 'fine'), None, 'model')
All inputs are finite; a program needn't handle non-finite values.
Results may differ from a plain program's by a relative error of at most 0.001.
Values may be sent and summed in bfloat16 or wider, within the bound.
A program may use at most 128 MiB of HBM per device.

v0:
```python
import jax
import jax.numpy as jnp
from jax import lax
from jax.sharding import PartitionSpec as P

PAGE = 32


def turn_pairs(vectors, angle):
    half = vectors.shape[-1] // 2
    cosine, sine = (jnp.cos(angle)[None, :, None, :], jnp.sin(angle)[None, :, None, :])
    first, second = (vectors[..., :half], vectors[..., half:])
    return jnp.concatenate(
        [first * cosine - second * sine, second * cosine + first * sine], axis=-1
    )


def prepare_keys(plain_keys, angle):
    wide_keys = plain_keys.astype(jnp.float32)
    return turn_pairs(wide_keys, angle)


def on_device(fresh_keys, fresh_values, turn_angle):
    my_angles = lax.dynamic_slice_in_dim(
        turn_angle, lax.axis_index(("coarse", "fine")) * fresh_keys.shape[1], fresh_keys.shape[1]
    )
    sent_keys = prepare_keys(fresh_keys, my_angles).astype(jnp.bfloat16)
    moved_keys, cache_values = (
        lax.all_to_all(sent_keys, ("coarse", "fine"), split_axis=0, concat_axis=1, tiled=True),
        lax.all_to_all(fresh_values, ("coarse", "fine"), split_axis=0, concat_axis=1, tiled=True),
    )
    page_view = moved_keys.reshape(
        moved_keys.shape[0], -1, PAGE, moved_keys.shape[2], moved_keys.shape[3]
    )
    page_high = jnp.max(page_view, axis=2)
    page_low = jnp.min(page_view, axis=2)
    return (moved_keys, cache_values, page_high, page_low)


def solution(mesh):
    return jax.shard_map(
        on_device,
        mesh=mesh,
        in_specs=(
            P(None, ("coarse", "fine"), "model", None),
            P(None, ("coarse", "fine"), "model", None),
            P(),
        ),
        out_specs=(
            P(("coarse", "fine"), None, "model", None),
            P(("coarse", "fine"), None, "model", None),
            P(("coarse", "fine"), None, "model", None),
            P(("coarse", "fine"), None, "model", None),
        ),
        check_vma=False,
    )
```

profile of v0, /device:TPU:0, one launch (start us, length us, event | category | flops | bytes accessed | tf_op | source)
XLA Modules:
  0.0 347.8 jit_solution(10292698317439789737)
XLA Ops:
  0.6 2.3 dynamic-slice_cosine_fusion
  3.0 0.3 copy.7
  3.2 0.3 copy.8
  3.5 6.7 %convert_element_type.4 = f32[8,1536,2,128]{3,2,1,0:T(2,128)S(1)} convert(bf16[8,1536,2,128]{3,2,1,0:T(2,128)(2,1)} %param.3) | non-fusion elementwise | flops 3145728 | bytes 18874368 | tf_op jit(solution)/shard_map/convert_element_type | solution.py:19
  10.2 17.5 %subtract_convert_fusion = (bf16[8,1536,2,64]{3,2,1,0:T(2,128)(2,1)S(1)}, bf16[8,1536,2,64]{3,2,1,0:T(2,128)(2,1)S(1)}) fusion(f32[8,1536,2,128]{3,2,1,0:T(2,128)S(1)} %convert_element_type.4, f32[1536,64]{1,0:T(8,128)S(1)} %copy.8, f32[1536,64]{1,0:T(8,128)S(1)} %copy.7), kind=kLoop, calls=%fused_computation.1 | loop fusion | flops 12582912 | bytes 19660800 | tf_op jit(solution)/shard_map/convert
  27.8 17.3 %pad_maximum_fusion = bf16[8,1536,2,128]{3,2,1,0:T(2,128)(2,1)S(1)} fusion(bf16[8,1536,2,64]{3,2,1,0:T(2,128)(2,1)S(1)} %get-tuple-element.7, bf16[8,1536,2,64]{3,2,1,0:T(2,128)(2,1)S(1)} %get-tuple-element.6), kind=kLoop, calls=%fused_computation.2 | loop fusion | flops 12582912 | bytes 12582912 | tf_op jit(solution)/shard_map/concatenate | solution.py:13
  45.0 146.4 %all_to_all.24 = bf16[8,1536,2,128]{3,2,1,0:T(2,128)(2,1)} all-to-all(bf16[8,1536,2,128]{3,2,1,0:T(2,128)(2,1)S(1)} %pad_maximum_fusion), channel_id=1, replica_groups=mesh['coarse'=2,'fine'=4,'model'=4] {'coarse','fine'}, dimensions={0} | all-to-all | bytes 12582912 | tf_op jit(solution)/shard_map/all_to_all | solution.py:29
  191.5 4.7 %all-to-all-start.1 = ((bf16[8,1536,2,128]{3,2,1,0:T(2,128)(2,1)}), bf16[8,1536,2,128]{3,2,1,0:T(2,128)(2,1)}, u32[]{:S(2)}, u32[]{:S(2)}) async-start(bf16[8,1536,2,128]{3,2,1,0:T(2,128)(2,1)} %param.4), calls=%async_computation.1 | async-start | bytes 12582912 | tf_op jit(solution)/shard_map/all_to_all | solution.py:30
  196.2 12.9 %fusion = (bf16[384,2,128]{2,1,0:T(2,128)(2,1)}, bf16[384,2,128]{2,1,0:T(2,128)(2,1)}) fusion(bf16[1,384,32,2,128]{4,3,2,1,0:T(2,128)(2,1)} %bitcast.5), kind=kLoop, calls=%fused_computation.5 | loop fusion | flops 6094848 | bytes 6684672 | tf_op jit(solution)/shard_map/reduce_min | solution.py:36
  209.1 125.2 %all-to-all-done.1 = bf16[8,1536,2,128]{3,2,1,0:T(2,128)(2,1)} async-done(((bf16[8,1536,2,128]{3,2,1,0:T(2,128)(2,1)}), bf16[8,1536,2,128]{3,2,1,0:T(2,128)(2,1)}, u32[]{:S(2)}, u32[]{:S(2)}) %all-to-all-start.1) | async-done | bytes 6291488 | tf_op jit(solution)/shard_map/all_to_all | solution.py:30
  334.3 6.7 %copy.11 = bf16[1,12288,2,128]{3,2,1,0:T(2,128)(2,1)} copy(bf16[1,12288,2,128]{3,2,1,0:T(2,128)(2,1)} %bitcast.6) | data formatting | bytes 12582912
  341.1 6.7 %copy.12 = bf16[1,12288,2,128]{3,2,1,0:T(2,128)(2,1)} copy(bf16[1,12288,2,128]{3,2,1,0:T(2,128)(2,1)} %bitcast.1) | data formatting | bytes 12582912
Async XLA Ops:
  191.5 142.9 %all-to-all-start.1 = ((bf16[8,1536,2,128]{3,2,1,0:T(2,128)(2,1)}), bf16[8,1536,2,128]{3,2,1,0:T(2,128)(2,1)}, u32[]{:S(2)}, u32[]{:S(2)}) async-start(bf16[8,1536,2,128]{3,2,1,0:T(2,128)(2,1)} %param.4), calls=%async_computation.1 | async-start | bytes 12582912 | tf_op jit(solution)/shard_map/all_to_all | solution.py:30
where the time goes:
time: 348 us
  blocking collectives  146 us (42%)
  waiting for transfers between devices  125 us (36%)
  other arithmetic  54.4 us (16%)
  local copies, waits for them, and re-layouts  16.3 us (5%)
  starting transfers between devices  4.74 us (1%)
    all_to_all x1, blocking collectives, on_device(): lax.all_to_all(sent_keys, ('coarse', 'fine'), split_axis=0, concat_axis=1...  146 us
    all_to_all x1, waiting for transfers between devices, on_device(): lax.all_to_all(fresh_values, ('coarse', 'fine'), split_axis=0, concat_axi...  125 us
    another operation x1, other arithmetic  17.5 us
    concatenate x1, other arithmetic, turn_pairs(): jnp.concatenate([first * cosine - second * sine, second * cosine + first...  17.3 us
    unnamed x2, local copies, waits for them, and re-layouts  13.4 us
    reduce_min x1, other arithmetic, on_device(): page_low = jnp.min(page_view, axis=2)  12.9 us
  transfers between devices with their start and end apart: 1, of which 1 were waited for; matrix products, arithmetic and copies ran while one was open for 4% of the time, Pallas kernels for 0%

commit v1 on v0

v1 whole, which is shorter than its diff:
```python
import functools

import jax
import jax.numpy as jnp
from jax import lax
from jax.experimental import pallas as pl
from jax.experimental.pallas import tpu as pltpu
from jax.sharding import PartitionSpec as P

PAGE = 32
BLOCK = 256
TILE = 16
AXES = ("coarse", "fine")
MESH = pl.DeviceIdType.MESH


def exchange_kernel(
    nc, nf, heads, keys, values, angles,
    got_keys, got_values, high, low,
    plain, turned, near_angles, cosine, sine, folded, paired,
    angle_sem, plain_sem, own_sem, key_send, key_recv, value_send, value_recv,
):
    n = nc * nf
    per, rows = keys.shape[0] // n, keys.shape[1]
    length, half = rows // heads, angles.shape[0]
    head_size = 2 * half
    mine_c, mine_f = lax.axis_index("coarse"), lax.axis_index("fine")
    me = mine_c * nf + mine_f
    my_rows = pl.ds(pl.multiple_of(me * rows, rows), rows)

    way = 1 - 2 * (mine_f // max(nf // 2, 1))

    def device(step_c, step_f):
        c = lax.rem(mine_c + step_c, nc)
        f = lax.rem(mine_f + way * step_f + nf, nf)
        return c, f, c * nf + f

    order = [(c, f) for f in list(range(1, nf)) for c in range(nc)]
    order[nc:nc] = [(c, 0) for c in range(1, nc)]
    early = nc

    angle_copy = pltpu.make_async_copy(
        angles.at[:, pl.ds(pl.multiple_of(me * length, length), length)], near_angles, angle_sem
    )
    angle_copy.start()

    def chunk_of(index):
        return pl.ds(index * per, per)

    def plain_copy(slot, index):
        return pltpu.make_async_copy(keys.at[chunk_of(index)], plain.at[slot], plain_sem.at[slot])

    partners = [device(*step) for step in order]
    for slot, (_, _, index) in enumerate(partners):
        plain_copy(slot, index).start()
    plain_copy(n - 1, me).start()

    barrier = pltpu.get_barrier_semaphore()
    for c, f, _ in partners:
        pl.semaphore_signal(barrier, inc=1, device_id={"coarse": c, "fine": f}, device_id_type=MESH)
    pl.semaphore_wait(barrier, n - 1)

    def send_values(slot):
        c, f, index = partners[slot]
        return pltpu.make_async_remote_copy(
            src_ref=values.at[chunk_of(index)],
            dst_ref=got_values.at[:, my_rows],
            send_sem=value_send.at[slot],
            recv_sem=value_recv.at[me],
            device_id={"coarse": c, "fine": f},
            device_id_type=MESH,
        )

    def send_keys(slot):
        c, f, _ = partners[slot]
        return pltpu.make_async_remote_copy(
            src_ref=turned.at[slot],
            dst_ref=got_keys.at[:, my_rows],
            send_sem=key_send.at[slot],
            recv_sem=key_recv.at[me],
            device_id={"coarse": c, "fine": f},
            device_id_type=MESH,
        )

    for slot in range(early):
        send_values(slot).start()
    own_copy = pltpu.make_async_copy(values.at[chunk_of(me)], got_values.at[:, my_rows], own_sem)
    own_copy.start()

    angle_copy.wait()
    cos_half = jnp.cos(near_angles[...]).T
    sin_half = jnp.sin(near_angles[...]).T
    cos_whole = jnp.concatenate([cos_half, cos_half], axis=1)
    sin_whole = jnp.concatenate([-sin_half, sin_half], axis=1)
    for h in range(heads):
        cosine[pl.ds(h, length, stride=heads), :] = cos_whole
        sine[pl.ds(h, length, stride=heads), :] = sin_whole

    def turn(slot, store):
        for s in range(per):
            @pl.loop(0, rows // BLOCK)
            def _(i):
                here = pl.ds(pl.multiple_of(i * BLOCK, BLOCK), BLOCK)
                wide = plain[slot, s, here, :].astype(jnp.float32)
                out = wide * cosine[here, :] + pltpu.roll(wide, half, 1) * sine[here, :]
                store(s, i, out.astype(jnp.bfloat16))

    def store_turned(slot):
        def store(s, i, block):
            turned[slot, s, pl.ds(pl.multiple_of(i * BLOCK, BLOCK), BLOCK), :] = block
        return store

    def store_own(s, i, block):
        got_keys[s, pl.ds(pl.multiple_of(me * rows + i * BLOCK, BLOCK), BLOCK), :] = block

    def prepare(slot, index):
        plain_copy(slot, index).wait()
        turn(slot, store_turned(slot))

    for slot in range(early):
        prepare(slot, partners[slot][2])
        if slot >= 1:
            send_keys(slot - 1).start()
    prepare(early, partners[early][2])
    send_keys(early - 1).start()
    for slot in range(early, n - 1):
        send_values(slot).start()
    for slot in range(early + 1, n - 1):
        prepare(slot, partners[slot][2])
        send_keys(slot - 1).start()
    plain_copy(n - 1, me).wait()
    turn(n - 1, store_own)
    send_keys(n - 2).start()

    pages = length // PAGE
    fold = PAGE * heads // TILE

    def bound(index, pick, out):
        for s in range(per):
            block = got_keys[s, pl.ds(pl.multiple_of(index * rows, rows), rows), :]
            tiles = block.reshape(pages, fold, TILE, head_size)
            best = tiles[:, 0]
            for t in range(1, fold):
                best = pick(best, tiles[:, t])
            folded[...] = best.astype(jnp.float32).reshape(pages * TILE, head_size)
            for h in range(heads):
                top = folded[pl.ds(h, pages, stride=TILE), :]
                for j in range(1, TILE // heads):
                    top = pick(top, folded[pl.ds(j * heads + h, pages, stride=TILE), :])
                paired[pl.ds(h, pages, stride=heads), :] = top
            span = pages * heads
            out[s, pl.ds(pl.multiple_of(index * span, span), span), :] = paired[...].astype(jnp.bfloat16)

    bound(me, jnp.maximum, high)
    bound(me, jnp.minimum, low)

    def arrived(buffer, sems, index):
        there = buffer.at[:, pl.ds(pl.multiple_of(index * rows, rows), rows)]
        return pltpu.make_async_copy(there, there, sems.at[index])

    def source(step_c, step_f):
        f = lax.rem(mine_f + step_f, nf)
        return lax.rem(mine_c + step_c, nc) * nf + f

    others = [source((nc - c) % nc, f) for f, c in [(f, c) for f in range(nf) for c in range(nc)][1:]]
    for index in others:
        arrived(got_keys, key_recv, index).wait()
        bound(index, jnp.maximum, high)
        bound(index, jnp.minimum, low)
    for index in others:
        arrived(got_values, value_recv, index).wait()
    own_copy.wait()
    for slot in range(n - 1):
        send_values(slot).wait_send()
        send_keys(slot).wait_send()


def write_kernel(*refs):
    count = len(refs) // 2
    sources, targets, sems = refs[:count], refs[count:2 * count], refs[2 * count]
    copies = [
        pltpu.make_async_copy(a, b, sems.at[i]) for i, (a, b) in enumerate(zip(sources, targets))
    ]
    for copy in copies:
        copy.start()
    for copy in copies:
        copy.wait()


def on_device(nc, nf, fresh_keys, fresh_values, turn_angle):
    batch, length, heads, size = fresh_keys.shape
    n, rows, half = nc * nf, length * heads, size // 2
    per = batch // n
    pages = length // PAGE
    keys = fresh_keys.reshape(batch, rows, size)
    values = fresh_values.reshape(batch, rows, size)
    whole = (per, n * rows, size)
    bounds = (per, n * pages * heads, size)
    vmem, anywhere = pl.BlockSpec(memory_space=pltpu.VMEM), pl.BlockSpec(memory_space=pl.ANY)
    arrived = pl.pallas_call(
        functools.partial(exchange_kernel, nc, nf, heads),
        out_shape=[pltpu.VMEM(shape, jnp.bfloat16) for shape in (whole, whole, bounds, bounds)],
        in_specs=[anywhere] * 3,
        out_specs=[vmem] * 4,
        scratch_shapes=[
            pltpu.VMEM((n, per, rows, size), jnp.bfloat16),
            pltpu.VMEM((n - 1, per, rows, size), jnp.bfloat16),
            pltpu.VMEM((half, length), jnp.float32),
            pltpu.VMEM((rows, size), jnp.float32),
            pltpu.VMEM((rows, size), jnp.float32),
            pltpu.VMEM((pages * TILE, size), jnp.float32),
            pltpu.VMEM((pages * heads, size), jnp.float32),
            pltpu.SemaphoreType.DMA(()),
            pltpu.SemaphoreType.DMA((n,)),
            pltpu.SemaphoreType.DMA(()),
            pltpu.SemaphoreType.DMA((n - 1,)),
            pltpu.SemaphoreType.DMA((n,)),
            pltpu.SemaphoreType.DMA((n - 1,)),
            pltpu.SemaphoreType.DMA((n,)),
        ],
        compiler_params=pltpu.CompilerParams(
            collective_id=0, has_side_effects=True, vmem_limit_bytes=40 * 2**20
        ),
        name="exchange",
    )(keys, values, turn_angle.T)
    out = pl.pallas_call(
        write_kernel,
        out_shape=[jax.ShapeDtypeStruct(a.shape, a.dtype) for a in arrived],
        in_specs=[vmem] * 4,
        out_specs=[anywhere] * 4,
        scratch_shapes=[pltpu.SemaphoreType.DMA((4,))],
        compiler_params=pltpu.CompilerParams(vmem_limit_bytes=2**20),
        name="write",
    )(*[pltpu.with_memory_space_constraint(a, pltpu.VMEM) for a in arrived])
    return tuple(a.reshape(per, -1, heads, size) for a in out)


def solution(mesh):
    where = P(AXES, None, "model", None)
    return jax.shard_map(
        functools.partial(on_device, mesh.shape["coarse"], mesh.shape["fine"]),
        mesh=mesh,
        in_specs=(P(None, AXES, "model", None), P(None, AXES, "model", None), P()),
        out_specs=(where, where, where, where),
        check_vma=False,
    )
```

time: 348 us -> 311 us (0.89)
  Pallas kernels: 0 us -> 310 us
  blocking collectives: 146 us -> 0 us
  waiting for transfers between devices: 125 us -> 0 us
  other arithmetic: 54.4 us -> 0 us
  local copies, waits for them, and re-layouts: 16.3 us -> 0 us
  starting transfers between devices: 4.74 us -> 0 us
    pallas_call x0 -> x2, Pallas kernels: none -> 310 us  [the longest x1 305 us: on_device(): pl.pallas_call(functools.partial(exchange_kernel, nc, nf, heads), out_sha...]
    all_to_all x1 -> x0, blocking collectives: 146 us -> none  [on_device(): lax.all_to_all(sent_keys, ('coarse', 'fine'), split_axis=0, concat_axis=1...]
    all_to_all x1 -> x0, waiting for transfers between devices: 125 us -> none  [on_device(): lax.all_to_all(fresh_values, ('coarse', 'fine'), split_axis=0, concat_axi...]
    another operation x1 -> x0, other arithmetic: 17.5 us -> none
    concatenate x1 -> x0, other arithmetic: 17.3 us -> none  [turn_pairs(): jnp.concatenate([first * cosine - second * sine, second * cosine + first...]
    unnamed x2 -> x0, local copies, waits for them, and re-layouts: 13.4 us -> none
    reduce_min x1 -> x0, other arithmetic: 12.9 us -> none  [on_device(): page_low = jnp.min(page_view, axis=2)]
    convert_element_type x1 -> x0, other arithmetic: 6.72 us -> none  [prepare_keys(): wide_keys = plain_keys.astype(jnp.float32)]
  transfers between devices with their start and end apart: 1 -> 0, of which waited for: 1 -> 0; matrix products, arithmetic and copies ran while one was open for 4% -> 0% of each run, Pallas kernels for 0% -> 0%
where the time goes in v1:
time: 311 us
  Pallas kernels  310 us (100%)
    pallas_call x1, Pallas kernels, on_device(): pl.pallas_call(functools.partial(exchange_kernel, nc, nf, heads), out_sha...  305 us

profile of v1, /device:TPU:0, one launch (start us, length us, event | category | flops | bytes accessed | tf_op | source)
XLA Modules:
  0.0 310.5 jit_solution(13617579052344929971)
XLA Ops:
  0.6 305.1 %exchange.1 = (bf16[1,24576,128]{2,1,0:T(8,128)(2,1)S(1)}, bf16[1,24576,128]{2,1,0:T(8,128)(2,1)S(1)}, bf16[1,768,128]{2,1,0:T(8,128)(2,1)S(1)}, bf16[1,768,128]{2,1,0:T(8,128)(2,1)S(1)}) custom-call(bf16[8,3072,128]{2,1,0:T(8,128)(2,1)} %bitcast.7, bf16[8,3072,128]{2,1,0:T(8,128)(2,1)} %bitcast.8, f32[64,12288]{1,0:T(8,128)} %bitcast.9), custom_call_target="tpu_custom_call" | custom-call | tf_op jit(solution)/shard_map/exchange/pallas_call | solution.py:200
  305.7 4.8 %write.1 = (bf16[1,24576,128]{2,1,0:T(8,128)(2,1)}, bf16[1,24576,128]{2,1,0:T(8,128)(2,1)}, bf16[1,768,128]{2,1,0:T(8,128)(2,1)}, bf16[1,768,128]{2,1,0:T(8,128)(2,1)}) custom-call(bf16[1,24576,128]{2,1,0:T(8,128)(2,1)S(1)} %get-tuple-element.12.refs_0_, bf16[1,24576,128]{2,1,0:T(8,128)(2,1)S(1)} %get-tuple-element.13.refs_1_, ...), custom_call_target="tpu_custom_call" | custom-call | tf_op jit(solution)/shard_map/write/pallas_call | solution.py:226

commit v2 on v1

--- a/solution.py
+++ b/solution.py
@@ -9,6 +9,7 @@
 
 PAGE = 32
 BLOCK = 256
+PIECE = 192
 TILE = 16
 AXES = ("coarse", "fine")
 MESH = pl.DeviceIdType.MESH
@@ -28,16 +29,11 @@
     me = mine_c * nf + mine_f
     my_rows = pl.ds(pl.multiple_of(me * rows, rows), rows)
 
-    way = 1 - 2 * (mine_f // max(nf // 2, 1))
+    order = [(c, f) for f in range(nf) for c in range(nc)][1:]
 
     def device(step_c, step_f):
-        c = lax.rem(mine_c + step_c, nc)
-        f = lax.rem(mine_f + way * step_f + nf, nf)
+        c, f = lax.rem(mine_c + step_c, nc), lax.rem(mine_f + step_f, nf)
         return c, f, c * nf + f
-
-    order = [(c, f) for f in list(range(1, nf)) for c in range(nc)]
-    order[nc:nc] = [(c, 0) for c in range(1, nc)]
-    early = nc
 
     angle_copy = pltpu.make_async_copy(
         angles.at[:, pl.ds(pl.multiple_of(me * length, length), length)], near_angles, angle_sem
@@ -60,30 +56,33 @@
         pl.semaphore_signal(barrier, inc=1, device_id={"coarse": c, "fine": f}, device_id_type=MESH)
     pl.semaphore_wait(barrier, n - 1)
 
-    def send_values(slot):
-        c, f, index = partners[slot]
+    def send(source, target, sends, recvs, slot, first, count):
+        c, f, _ = partners[slot]
         return pltpu.make_async_remote_copy(
-            src_ref=values.at[chunk_of(index)],
-            dst_ref=got_values.at[:, my_rows],
-            send_sem=value_send.at[slot],
-            recv_sem=value_recv.at[me],
+            src_ref=source.at[:, pl.ds(first, count)],
+            dst_ref=target.at[:, pl.ds(pl.multiple_of(me * rows + first, PIECE), count)],
+            send_sem=sends.at[slot],
+            recv_sem=recvs.at[me],
             device_id={"coarse": c, "fine": f},
             device_id_type=MESH,
         )
 
-    def send_keys(slot):
-        c, f, _ = partners[slot]
-        return pltpu.make_async_remote_copy(
-            src_ref=turned.at[slot],
-            dst_ref=got_keys.at[:, my_rows],
-            send_sem=key_send.at[slot],
-            recv_sem=key_recv.at[me],
-            device_id={"coarse": c, "fine": f},
-            device_id_type=MESH,
-        )
-
-    for slot in range(early):
-        send_values(slot).start()
+    def send_values(slot, first, count):
+        source = values.at[chunk_of(partners[slot][2])]
+        return send(source, got_values, value_send, value_recv, slot, first, count)
+
+    def send_keys(slot, first, count):
+        return send(turned.at[slot], got_keys, key_send, key_recv, slot, first, count)
+
+    pieces = rows // PIECE
+
+    def send_pieces(send_one, first, last):
+        @pl.loop(first, last)
+        def _(p):
+            for slot in range(n - 1):
+                send_one(slot, pl.multiple_of(p * PIECE, PIECE), PIECE).start()
+
+    send_pieces(send_values, 0, pieces // 2)
     own_copy = pltpu.make_async_copy(values.at[chunk_of(me)], got_values.at[:, my_rows], own_sem)
     own_copy.start()
 
@@ -113,24 +112,13 @@
     def store_own(s, i, block):
         got_keys[s, pl.ds(pl.multiple_of(me * rows + i * BLOCK, BLOCK), BLOCK), :] = block
 
-    def prepare(slot, index):
+    for slot, (_, _, index) in enumerate(partners):
         plain_copy(slot, index).wait()
         turn(slot, store_turned(slot))
-
-    for slot in range(early):
-        prepare(slot, partners[slot][2])
-        if slot >= 1:
-            send_keys(slot - 1).start()
-    prepare(early, partners[early][2])
-    send_keys(early - 1).start()
-    for slot in range(early, n - 1):
-        send_values(slot).start()
-    for slot in range(early + 1, n - 1):
-        prepare(slot, partners[slot][2])
-        send_keys(slot - 1).start()
     plain_copy(n - 1, me).wait()
     turn(n - 1, store_own)
-    send_keys(n - 2).start()
+    send_pieces(send_keys, 0, pieces)
+    send_pieces(send_values, pieces // 2, pieces)
 
     pages = length // PAGE
     fold = PAGE * heads // TILE
@@ -158,11 +146,7 @@
         there = buffer.at[:, pl.ds(pl.multiple_of(index * rows, rows), rows)]
         return pltpu.make_async_copy(there, there, sems.at[index])
 
-    def source(step_c, step_f):
-        f = lax.rem(mine_f + step_f, nf)
-        return lax.rem(mine_c + step_c, nc) * nf + f
-
-    others = [source((nc - c) % nc, f) for f, c in [(f, c) for f in range(nf) for c in range(nc)][1:]]
+    others = [device((nc - c) % nc, (nf - f) % nf)[2] for c, f in order]
     for index in others:
         arrived(got_keys, key_recv, index).wait()
         bound(index, jnp.maximum, high)
@@ -171,8 +155,8 @@
         arrived(got_values, value_recv, index).wait()
     own_copy.wait()
     for slot in range(n - 1):
-        send_values(slot).wait_send()
-        send_keys(slot).wait_send()
+        send_values(slot, 0, rows).wait_send()
+        send_keys(slot, 0, rows).wait_send()
 
 
 def write_kernel(*refs):

time: 311 us -> 281 us (0.904)
  Pallas kernels: 310 us -> 280 us
    pallas_call x1, Pallas kernels: 305 us -> 275 us  [on_device(): pl.pallas_call(functools.partial(exchange_kernel, nc, nf, heads), out_sha...]
where the time goes in v2:
time: 281 us
  Pallas kernels  280 us (100%)
    pallas_call x1, Pallas kernels, on_device(): pl.pallas_call(functools.partial(exchange_kernel, nc, nf, heads), out_sha...  275 us

profile of v2, /device:TPU:0, one launch (start us, length us, event | category | flops | bytes accessed | tf_op | source)
XLA Modules:
  0.0 280.7 jit_solution(13173897901208538779)
XLA Ops:
  0.6 275.2 %exchange.1 = (bf16[1,24576,128]{2,1,0:T(8,128)(2,1)S(1)}, bf16[1,24576,128]{2,1,0:T(8,128)(2,1)S(1)}, bf16[1,768,128]{2,1,0:T(8,128)(2,1)S(1)}, bf16[1,768,128]{2,1,0:T(8,128)(2,1)S(1)}) custom-call(bf16[8,3072,128]{2,1,0:T(8,128)(2,1)} %bitcast.7, bf16[8,3072,128]{2,1,0:T(8,128)(2,1)} %bitcast.8, f32[64,12288]{1,0:T(8,128)} %bitcast.9), custom_call_target="tpu_custom_call" | custom-call | tf_op jit(solution)/shard_map/exchange/pallas_call | solution.py:184
  275.9 4.8 %write.1 = (bf16[1,24576,128]{2,1,0:T(8,128)(2,1)}, bf16[1,24576,128]{2,1,0:T(8,128)(2,1)}, bf16[1,768,128]{2,1,0:T(8,128)(2,1)}, bf16[1,768,128]{2,1,0:T(8,128)(2,1)}) custom-call(bf16[1,24576,128]{2,1,0:T(8,128)(2,1)S(1)} %get-tuple-element.12.refs_0_, bf16[1,24576,128]{2,1,0:T(8,128)(2,1)S(1)} %get-tuple-element.13.refs_1_, ...), custom_call_target="tpu_custom_call" | custom-call | tf_op jit(solution)/shard_map/write/pallas_call | solution.py:210

commit v3 on v2

--- a/solution.py
+++ b/solution.py
@@ -10,6 +10,7 @@
 PAGE = 32
 BLOCK = 256
 PIECE = 192
+LAST_PIECE = 48
 TILE = 16
 AXES = ("coarse", "fine")
 MESH = pl.DeviceIdType.MESH
@@ -60,7 +61,7 @@
         c, f, _ = partners[slot]
         return pltpu.make_async_remote_copy(
             src_ref=source.at[:, pl.ds(first, count)],
-            dst_ref=target.at[:, pl.ds(pl.multiple_of(me * rows + first, PIECE), count)],
+            dst_ref=target.at[:, pl.ds(pl.multiple_of(me * rows + first, LAST_PIECE), count)],
             send_sem=sends.at[slot],
             recv_sem=recvs.at[me],
             device_id={"coarse": c, "fine": f},
@@ -76,11 +77,11 @@
 
     pieces = rows // PIECE
 
-    def send_pieces(send_one, first, last):
-        @pl.loop(first, last)
+    def send_pieces(send_one, first, last, size=PIECE):
+        @pl.loop(first * (PIECE // size), last * (PIECE // size))
         def _(p):
             for slot in range(n - 1):
-                send_one(slot, pl.multiple_of(p * PIECE, PIECE), PIECE).start()
+                send_one(slot, pl.multiple_of(p * size, size), size).start()
 
     send_pieces(send_values, 0, pieces // 2)
     own_copy = pltpu.make_async_copy(values.at[chunk_of(me)], got_values.at[:, my_rows], own_sem)
@@ -118,7 +119,8 @@
     plain_copy(n - 1, me).wait()
     turn(n - 1, store_own)
     send_pieces(send_keys, 0, pieces)
-    send_pieces(send_values, pieces // 2, pieces)
+    send_pieces(send_values, pieces // 2, pieces - 2)
+    send_pieces(send_values, pieces - 2, pieces, LAST_PIECE)
 
     pages = length // PAGE
     fold = PAGE * heads // TILE

time: 281 us -> 282 us (level)
  no operation moved by 1% of the time
where the time goes in v3:
time: 282 us
  Pallas kernels  282 us (100%)
    pallas_call x1, Pallas kernels, on_device(): pl.pallas_call(functools.partial(exchange_kernel, nc, nf, heads), out_sha...  277 us

profile of v3, /device:TPU:0, one launch (start us, length us, event | category | flops | bytes accessed | tf_op | source)
XLA Modules:
  0.0 282.3 jit_solution(12038187149507582462)
XLA Ops:
  0.6 276.8 %exchange.1 = (bf16[1,24576,128]{2,1,0:T(8,128)(2,1)S(1)}, bf16[1,24576,128]{2,1,0:T(8,128)(2,1)S(1)}, bf16[1,768,128]{2,1,0:T(8,128)(2,1)S(1)}, bf16[1,768,128]{2,1,0:T(8,128)(2,1)S(1)}) custom-call(bf16[8,3072,128]{2,1,0:T(8,128)(2,1)} %bitcast.7, bf16[8,3072,128]{2,1,0:T(8,128)(2,1)} %bitcast.8, f32[64,12288]{1,0:T(8,128)} %bitcast.9), custom_call_target="tpu_custom_call" | custom-call | tf_op jit(solution)/shard_map/exchange/pallas_call | solution.py:186
  277.5 4.8 %write.1 = (bf16[1,24576,128]{2,1,0:T(8,128)(2,1)}, bf16[1,24576,128]{2,1,0:T(8,128)(2,1)}, bf16[1,768,128]{2,1,0:T(8,128)(2,1)}, bf16[1,768,128]{2,1,0:T(8,128)(2,1)}) custom-call(bf16[1,24576,128]{2,1,0:T(8,128)(2,1)S(1)} %get-tuple-element.12.refs_0_, bf16[1,24576,128]{2,1,0:T(8,128)(2,1)S(1)} %get-tuple-element.13.refs_1_, ...), custom_call_target="tpu_custom_call" | custom-call | tf_op jit(solution)/shard_map/write/pallas_call | solution.py:212
